TPU v7x, 128 devices: a whole 4x4x4 slice. The times are simulated.
128 devices in a mesh: data: 1, expert: 128 (over z, y, x, core).
Axes of the slice: x: 4, y: 4, z: 4, core: 2. Of those that a mesh axis runs over, the one named last changes fastest.
Arguments:
- token_rows: bfloat16 [65536, 1024], P(('data', 'expert'))
- expert_ids: int32 [65536, 2], P(('data', 'expert'))
- gate_weights: float32 [65536, 2], P(('data', 'expert'))
- w_in: bfloat16 [128, 1024, 1024], P('expert')
- w_out: bfloat16 [128, 1024, 1024], P('expert')
Outputs:
- output: bfloat16 [65536, 1024], P(('data', 'expert'))
All inputs are finite; a program needn't handle non-finite values.
Results may differ from a plain program's by a relative error of at most 0.001.
Values are sent between devices in bfloat16 or wider.
A program may use at most 1 GiB of HBM per device.

v0:
```python
import jax
import jax.numpy as jnp
from jax import lax
from jax.sharding import PartitionSpec as P


def route_local(expert_ids, experts):
    ids_t = expert_ids.T
    onehot = (ids_t[:, :, None] == jnp.arange(experts, dtype=jnp.int32)).astype(jnp.int32)
    running = jnp.cumsum(onehot, axis=1)
    counts = running[:, -1, :]
    rank_local = jnp.sum(onehot * running, axis=2) - 1
    return ids_t, counts, rank_local


def solution(mesh):
    groups = mesh.shape["expert"]
    row_spec = P(("data", "expert"), None)
    weight_spec = P("expert", None, None)

    def device_step(token_rows, expert_ids, gate_weights, w_in, w_out):
        tokens, top_k = expert_ids.shape
        local_experts, model_dim = w_in.shape[0], w_in.shape[1]
        experts = local_experts * groups
        mean_load = tokens * top_k // experts
        send_cap = 7 * mean_load // 4
        capacity = groups * mean_load
        rows_total = experts * send_cap
        ids_t, counts, rank_local = route_local(expert_ids, experts)
        inclusive = counts
        shift = 1
        while shift < groups:
            pairs_list = [(source, source + shift) for source in range(groups - shift)]
            inclusive = inclusive + lax.ppermute(inclusive, "expert", pairs_list)
            shift = shift * 2
        before = inclusive - counts
        totals = lax.psum(counts, "expert")
        prior = jnp.cumsum(totals, axis=0) - totals
        within = jnp.cumsum(counts, axis=0) - counts
        slot = jnp.take_along_axis(prior + before, ids_t, axis=1) + rank_local
        keep = slot < capacity
        target = ids_t * send_cap + jnp.take_along_axis(within, ids_t, axis=1) + rank_local
        token_ids = jnp.broadcast_to(jnp.arange(tokens, dtype=jnp.int32), (top_k, tokens))
        source_row = jnp.full((rows_total,), tokens, jnp.int32).at[jnp.where(keep, target, rows_total).reshape(-1)].set(token_ids.reshape(-1), mode="drop")
        padded = jnp.concatenate([token_rows, jnp.zeros((1, model_dim), token_rows.dtype)], axis=0)
        outbound = jnp.take(padded, source_row, axis=0).reshape(experts, send_cap, model_dim)
        inbound = lax.all_to_all(outbound, "expert", 0, 0, tiled=True).reshape(groups, local_experts, send_cap, model_dim)
        pre_act = jnp.einsum("gesd,edf->gesf", inbound, w_in, preferred_element_type=jnp.float32)
        hidden = jax.nn.gelu(pre_act).astype(jnp.bfloat16)
        expert_out = jnp.einsum("gesf,efd->gesd", hidden, w_out, preferred_element_type=jnp.float32).astype(jnp.bfloat16)
        returned = lax.all_to_all(expert_out.reshape(experts, send_cap, model_dim), "expert", 0, 0, tiled=True).reshape(rows_total, model_dim)
        picked = jnp.take(returned, target, axis=0)
        weight = jnp.where(keep, gate_weights.T, 0.0)
        mixed = jnp.sum(weight[:, :, None] * picked.astype(jnp.float32), axis=0)
        return (token_rows.astype(jnp.float32) + mixed).astype(jnp.bfloat16)

    return jax.shard_map(device_step, mesh=mesh, in_specs=(row_spec, row_spec, row_spec, weight_spec, weight_spec), out_specs=row_spec, check_vma=False)
```

profile of v0, /device:TPU:0, one launch (start us, length us, event | category | flops | bytes accessed | tf_op | source)
XLA Modules:
  0.0 328.9 jit_solution(5390076400840680198)
XLA Ops:
  0.0 0.0 copy-start
  0.0 0.8 eq.23
  0.9 0.1 copy.12
  1.0 0.4 fusion.29
  1.5 0.1 broadcast_add_fusion
  1.7 1.3 collective-permute-start
  3.0 0.8 collective-permute-done
  3.8 6.3 %collective-permute-start.1 = (s32[2,128]{1,0:T(2,128)S(1)}, s32[2,128]{1,0:T(2,128)S(1)}, u32[]{:S(2)}, u32[]{:S(2)}) collective-permute-start(s32[2,128]{1,0:T(2,128)S(1)} %add.85), channel_id=1, source_target_pairs={{0,2},{1,3},{2,4},{3,5},{4,6},{5,7},{6,8},{7,9},{8,10},{9,11},{10,... | collective-permute-start | bytes 3080 | tf_op jit(solution)/shard_map/ppermute | solution.py:34
  10.1 1.3 collective-permute-done.1
  11.4 5.7 %collective-permute-start.2 = (s32[2,128]{1,0:T(2,128)S(1)}, s32[2,128]{1,0:T(2,128)S(1)}, u32[]{:S(2)}, u32[]{:S(2)}) collective-permute-start(s32[2,128]{1,0:T(2,128)S(1)} %add.86), channel_id=1, source_target_pairs={{0,4},{1,5},{2,6},{3,7},{4,8},{5,9},{6,10},{7,11},{8,12},{9,13},{1... | collective-permute-start | bytes 3080 | tf_op jit(solution)/shard_map/ppermute | solution.py:34
  17.1 1.3 collective-permute-done.2
  18.4 9.3 %collective-permute-start.3 = (s32[2,128]{1,0:T(2,128)S(1)}, s32[2,128]{1,0:T(2,128)S(1)}, u32[]{:S(2)}, u32[]{:S(2)}) collective-permute-start(s32[2,128]{1,0:T(2,128)S(1)} %add.87), channel_id=1, source_target_pairs={{0,8},{1,9},{2,10},{3,11},{4,12},{5,13},{6,14},{7,15},{8,16},{9,17... | collective-permute-start | bytes 3080 | tf_op jit(solution)/shard_map/ppermute | solution.py:34
  27.7 1.3 collective-permute-done.3
  29.0 5.8 %collective-permute-start.4 = (s32[2,128]{1,0:T(2,128)S(1)}, s32[2,128]{1,0:T(2,128)S(1)}, u32[]{:S(2)}, u32[]{:S(2)}) collective-permute-start(s32[2,128]{1,0:T(2,128)S(1)} %add.88), channel_id=1, source_target_pairs={{0,16},{1,17},{2,18},{3,19},{4,20},{5,21},{6,22},{7,23},{8,24},{9,... | collective-permute-start | bytes 3080 | tf_op jit(solution)/shard_map/ppermute | solution.py:34
  34.8 0.7 fusion.32
  35.5 0.6 collective-permute-done.4
  36.1 13.7 %collective-permute-start.5 = (s32[2,128]{1,0:T(2,128)S(1)}, s32[2,128]{1,0:T(2,128)S(1)}, u32[]{:S(2)}, u32[]{:S(2)}) collective-permute-start(s32[2,128]{1,0:T(2,128)S(1)} %add.89), channel_id=1, source_target_pairs={{0,32},{1,33},{2,34},{3,35},{4,36},{5,37},{6,38},{7,39},{8,40},{9,... | collective-permute-start | bytes 3080 | tf_op jit(solution)/shard_map/ppermute | solution.py:34
  49.8 1.1 select_reduce_fusion
  50.9 0.2 collective-permute-done.5
  51.1 6.1 %collective-permute-start.6 = (s32[2,128]{1,0:T(2,128)S(1)}, s32[2,128]{1,0:T(2,128)S(1)}, u32[]{:S(2)}, u32[]{:S(2)}) collective-permute-start(s32[2,128]{1,0:T(2,128)S(1)} %add.90), channel_id=1, source_target_pairs={{0,64},{1,65},{2,66},{3,67},{4,68},{5,69},{6,70},{7,71},{8,72},{9,... | collective-permute-start | bytes 3080 | tf_op jit(solution)/shard_map/ppermute | solution.py:34
  57.3 62.5 %psum.7 = s32[2,128]{1,0:T(2,128)S(1)} all-reduce(s32[2,128]{1,0:T(2,128)S(1)} %bitcast.79), channel_id=1, replica_groups=mesh['data'=1,'expert'=128] {'expert'}, use_global_device_ids=true, to_apply=%region_2.3 | all-reduce | flops 256 | bytes 2048 | tf_op jit(solution)/shard_map/psum | solution.py:37
  119.8 1.3 concatenate.3
  121.1 0.0 collective-permute-done.6
  121.2 0.0 copy-start.2
  121.2 0.0 copy-start.3
  121.2 8.8 %gather_fusion.3 = s32[1024]{0:T(1024)S(1)} fusion(s32[2,128]{1,0:T(2,128)S(1)} %get-tuple-element.12, s32[1024]{0:T(1024)S(1)} %bitcast.70), kind=kCustom, calls=%fused_computation.1.clone | custom fusion | bytes 16384 | tf_op jit(solution)/shard_map/jit(take_along_axis)/gather | solution.py:42
  130.0 8.8 %gather_fusion.2 = s32[1024]{0:T(1024)S(1)} fusion(s32[2,128]{1,0:T(2,128)S(1)} %get-tuple-element.13, s32[1024]{0:T(1024)S(1)} %bitcast.71), kind=kCustom, calls=%fused_computation.clone | custom fusion | bytes 16384 | tf_op jit(solution)/shard_map/jit(take_along_axis)/gather | solution.py:40
  138.7 0.0 copy-done.2
  138.8 0.0 copy-done.3
  138.9 4.3 %scatter_custom_fusion = s32[1792]{0:T(1024)S(1)} fusion(s32[1024]{0:T(1024)S(1)} %bitcast.84, s32[1024]{0:T(1024)S(1)} %bitcast.83, s32[]{:T(128)} %constant.44.clone.1), kind=kCustom, calls=%fused_computation.52 | custom fusion | bytes 7172 | tf_op jit(solution)/shard_map/scatter | solution.py:44
  143.2 0.1 broadcast_in_dim.50
  143.4 6.6 %gather_fusion = bf16[1792,1024]{1,0:T(8,128)(2,1)} fusion(bf16[513,1024]{1,0:T(8,128)(2,1)S(1)} %concatenate.3, s32[2048]{0:T(1024)S(1)} %pad_clamp_fusion), kind=kCustom, calls=%fused_computation.2 | custom fusion | bytes 7347200 | tf_op jit(solution)/shard_map/jit(_take)/gather | solution.py:46
  150.0 6.4 %gather.14 = bf16[128,14,1024]{2,1,0:T(8,128)(2,1)} reshape(bf16[1792,1024]{1,0:T(8,128)(2,1)} %gather_fusion) | data formatting | bytes 7340032 | tf_op jit(solution)/shard_map/jit(_take)/gather | solution.py:46
  156.3 2.5 broadcast_select_fusion
  158.8 62.9 %all_to_all.10 = bf16[128,14,1024]{2,1,0:T(8,128)(2,1)} all-to-all(bf16[128,14,1024]{2,1,0:T(8,128)(2,1)S(1)} %broadcast_select_fusion), channel_id=1, replica_groups=mesh['data'=1,'expert'=128] {'expert'}, dimensions={0} | all-to-all | bytes 7340032 | tf_op jit(solution)/shard_map/all_to_all | solution.py:47
  221.7 0.0 copy-done
  221.7 13.3 %fusion.16 = bf16[128,14,1024]{2,0,1:T(8,128)(2,1)} fusion(bf16[1,1024,1024]{2,1,0:T(8,128)(2,1)S(1)} %copy-done, bf16[128,14,1024]{2,1,0:T(8,128)(2,1)} %all_to_all.10, bf16[1,1024,1024]{2,1,0:T(8,128)(2,1)} %param.10), kind=kOutput, calls=%fused_computation.23 | convolution fusion | flops 7534542848 | bytes 11534336 | tf_op jit(solution)/shard_map/gesf,efd->gesd/dot_general | solution.py:50
  235.1 6.1 %copy.15 = bf16[128,14,1024]{2,1,0:T(8,128)(2,1)} copy(bf16[128,14,1024]{2,0,1:T(8,128)(2,1)} %fusion.16) | data formatting | bytes 7340032 | tf_op jit(solution)/shard_map/convert_element_type | solution.py:50
  241.1 8.8 %all-to-all-start.1 = ((bf16[128,14,1024]{2,1,0:T(8,128)(2,1)}), bf16[128,14,1024]{2,1,0:T(8,128)(2,1)}, u32[]{:S(2)}, u32[]{:S(2)}) async-start(bf16[128,14,1024]{2,1,0:T(8,128)(2,1)} %copy.15), calls=%async_computation.1 | async-start | bytes 8388608 | tf_op jit(solution)/shard_map/all_to_all | solution.py:51
  250.0 60.1 %all-to-all-done.1 = bf16[128,14,1024]{2,1,0:T(8,128)(2,1)} async-done(((bf16[128,14,1024]{2,1,0:T(8,128)(2,1)}), bf16[128,14,1024]{2,1,0:T(8,128)(2,1)}, u32[]{:S(2)}, u32[]{:S(2)}) %all-to-all-start.1) | async-done | bytes 3670048 | tf_op jit(solution)/shard_map/all_to_all | solution.py:51
  310.1 6.4 %reshape.97 = bf16[1792,1024]{1,0:T(8,128)(2,1)} reshape(bf16[128,14,1024]{2,1,0:T(8,128)(2,1)} %all-to-all-done.1) | data formatting | bytes 7340032 | tf_op jit(solution)/shard_map/reshape | solution.py:51
  316.5 8.5 %gather_fusion.1 = bf16[1024,1024]{1,0:T(8,128)(2,1)} fusion(bf16[1792,1024]{1,0:T(8,128)(2,1)} %reshape.97, s32[1024]{0:T(1024)S(1)} %broadcast_clamp_fusion), kind=kCustom, calls=%fused_computation.3 | custom fusion | bytes 4198400 | tf_op jit(solution)/shard_map/jit(_take)/gather | solution.py:52
  325.1 0.0 copy-start.1
  325.1 2.4 multiply_reduce_fusion
  327.5 0.0 copy-done.1
  327.5 1.3 add_convert_fusion
  (29 shorter events, 0.3 us)
Async XLA Ops:
  0.0 221.7 %copy-start = (bf16[1,1024,1024]{2,1,0:T(8,128)(2,1)S(1)}, bf16[1,1024,1024]{2,1,0:T(8,128)(2,1)}, u32[]{:S(2)}) copy-start(bf16[1,1024,1024]{2,1,0:T(8,128)(2,1)} %param.11) | copy-start | bytes 6291460
  1.7 2.1 collective-permute-start
  3.8 7.6 %collective-permute-start.1 = (s32[2,128]{1,0:T(2,128)S(1)}, s32[2,128]{1,0:T(2,128)S(1)}, u32[]{:S(2)}, u32[]{:S(2)}) collective-permute-start(s32[2,128]{1,0:T(2,128)S(1)} %add.85), channel_id=1, source_target_pairs={{0,2},{1,3},{2,4},{3,5},{4,6},{5,7},{6,8},{7,9},{8,10},{9,11},{10,... | collective-permute-start | bytes 3080 | tf_op jit(solution)/shard_map/ppermute | solution.py:34
  11.4 7.0 %collective-permute-start.2 = (s32[2,128]{1,0:T(2,128)S(1)}, s32[2,128]{1,0:T(2,128)S(1)}, u32[]{:S(2)}, u32[]{:S(2)}) collective-permute-start(s32[2,128]{1,0:T(2,128)S(1)} %add.86), channel_id=1, source_target_pairs={{0,4},{1,5},{2,6},{3,7},{4,8},{5,9},{6,10},{7,11},{8,12},{9,13},{1... | collective-permute-start | bytes 3080 | tf_op jit(solution)/shard_map/ppermute | solution.py:34
  18.4 10.6 %collective-permute-start.3 = (s32[2,128]{1,0:T(2,128)S(1)}, s32[2,128]{1,0:T(2,128)S(1)}, u32[]{:S(2)}, u32[]{:S(2)}) collective-permute-start(s32[2,128]{1,0:T(2,128)S(1)} %add.87), channel_id=1, source_target_pairs={{0,8},{1,9},{2,10},{3,11},{4,12},{5,13},{6,14},{7,15},{8,16},{9,17... | collective-permute-start | bytes 3080 | tf_op jit(solution)/shard_map/ppermute | solution.py:34
  29.0 7.1 %collective-permute-start.4 = (s32[2,128]{1,0:T(2,128)S(1)}, s32[2,128]{1,0:T(2,128)S(1)}, u32[]{:S(2)}, u32[]{:S(2)}) collective-permute-start(s32[2,128]{1,0:T(2,128)S(1)} %add.88), channel_id=1, source_target_pairs={{0,16},{1,17},{2,18},{3,19},{4,20},{5,21},{6,22},{7,23},{8,24},{9,... | collective-permute-start | bytes 3080 | tf_op jit(solution)/shard_map/ppermute | solution.py:34
  36.1 15.0 %collective-permute-start.5 = (s32[2,128]{1,0:T(2,128)S(1)}, s32[2,128]{1,0:T(2,128)S(1)}, u32[]{:S(2)}, u32[]{:S(2)}) collective-permute-start(s32[2,128]{1,0:T(2,128)S(1)} %add.89), channel_id=1, source_target_pairs={{0,32},{1,33},{2,34},{3,35},{4,36},{5,37},{6,38},{7,39},{8,40},{9,... | collective-permute-start | bytes 3080 | tf_op jit(solution)/shard_map/ppermute | solution.py:34
  51.1 70.0 %collective-permute-start.6 = (s32[2,128]{1,0:T(2,128)S(1)}, s32[2,128]{1,0:T(2,128)S(1)}, u32[]{:S(2)}, u32[]{:S(2)}) collective-permute-start(s32[2,128]{1,0:T(2,128)S(1)} %add.90), channel_id=1, source_target_pairs={{0,64},{1,65},{2,66},{3,67},{4,68},{5,69},{6,70},{7,71},{8,72},{9,... | collective-permute-start | bytes 3080 | tf_op jit(solution)/shard_map/ppermute | solution.py:34
  121.2 17.6 %copy-start.2 = (s32[512,2]{0,1:T(2,128)S(1)}, s32[512,2]{0,1:T(2,128)}, u32[]{:S(2)}) copy-start(s32[512,2]{0,1:T(2,128)} %param.8) | copy-start | bytes 12292
  121.2 17.6 %copy-start.3 = (f32[512,2]{0,1:T(2,128)S(1)}, f32[512,2]{0,1:T(2,128)}, u32[]{:S(2)}) copy-start(f32[512,2]{0,1:T(2,128)} %param.9) | copy-start | bytes 12292
  241.1 69.0 %all-to-all-start.1 = ((bf16[128,14,1024]{2,1,0:T(8,128)(2,1)}), bf16[128,14,1024]{2,1,0:T(8,128)(2,1)}, u32[]{:S(2)}, u32[]{:S(2)}) async-start(bf16[128,14,1024]{2,1,0:T(8,128)(2,1)} %copy.15), calls=%async_computation.1 | async-start | bytes 8388608 | tf_op jit(solution)/shard_map/all_to_all | solution.py:51
  325.1 2.5 copy-start.1
where the time goes:
time: 330 us; the launch traced here: 329 us
  blocking collectives  125 us (38%)
  waiting for transfers between devices  65.6 us (20%)
  local copies, waits for them, and re-layouts  58.4 us (18%)
  starting transfers between devices  57.1 us (17%)
  matrix products  13.3 us (4%)
  other arithmetic  8.78 us (3%)
    all_to_all x1, blocking collectives, device_step(): lax.all_to_all(outbound, 'expert', 0, 0, tiled=True)  62.9 us
    psum x1, blocking collectives, device_step(): totals = lax.psum(counts, 'expert')  62.5 us
    all_to_all x1, waiting for transfers between devices, device_step(): lax.all_to_all(expert_out.reshape(experts, send_cap, model_dim), 'expert'...  60.1 us
    ppermute x7, starting transfers between devices, device_step(): inclusive = inclusive + lax.ppermute(inclusive, 'expert', pairs_list)  48.3 us
    dot_general x1, matrix products, device_step(): jnp.einsum('gesf,efd->gesd', hidden, w_out, preferred_element_type=jnp.fl...  13.3 us
    gather x2, local copies, waits for them, and re-layouts, device_step(): jnp.take(padded, source_row, axis=0).reshape(experts, send_cap, model_dim)  13 us
    all_to_all x1, starting transfers between devices, device_step(): lax.all_to_all(expert_out.reshape(experts, send_cap, model_dim), 'expert'...  8.79 us
    gather x2, local copies, waits for them, and re-layouts, device_step(): slot = jnp.take_along_axis(prior + before, ids_t, axis=1) + rank_local  8.77 us
  transfers between devices with their start and end apart: 8, of which 7 were waited for; matrix products, arithmetic and copies ran while one was open for 1% of the time, Pallas kernels for 0%

commit v1 on v0

v1 whole, which is shorter than its diff:
```python
import functools

import jax
import jax.numpy as jnp
from jax import lax
from jax.experimental import pallas as pl
from jax.experimental.pallas import tpu as pltpu
from jax.sharding import PartitionSpec as P

SLOTS = 14
WIRE_ROWS = 16
BF16 = jnp.bfloat16
F32 = jnp.float32
I32 = jnp.int32


def moe_kernel(dims, capacity, ids_row, ids_col, gates, x, win_hbm, wout_hbm, out,
               outbuf, inbuf, obuf, retbuf, cbuf, win, wout, st, xs, hs, acc0, acc1, tmat, tinv, rrow, rcol, wcol,
               w_sem, c_send, c_recv, d_send, d_recv, r_send, r_recv):
    nz, ny, nx, nk = dims
    n = nz * ny * nx * nk
    nc, ng = nz * ny, nx * nk
    tokens, model = x.shape
    hidden = win.shape[1]
    dense = SLOTS * nc
    wire = WIRE_ROWS * nc
    half, quarter, eighth = model // 2, model // 4, model // 8
    width = SLOTS * model // WIRE_ROWS
    me = lax.axis_index("expert")
    mk = me % nk
    mx = (me // nk) % nx
    my = (me // (nk * nx)) % ny
    mz = me // (nk * nx * ny)

    def peer(g, c, sign):
        dx, dk, dz, dy = g // nk, g % nk, c // ny, c % ny
        z = (mz + nz + sign * dz) % nz
        y = (my + ny + sign * dy) % ny
        xx = (mx + nx + sign * dx) % nx
        k = (mk + nk + sign * dk) % nk
        return ((z * ny + y) * nx + xx) * nk + k

    def chunk_copy(src, dst, ssem, rsem, g, c, sign):
        rows = pl.ds(pl.multiple_of(g * wire + c * WIRE_ROWS, WIRE_ROWS), WIRE_ROWS)
        return pltpu.make_async_remote_copy(src_ref=src.at[rows], dst_ref=dst.at[rows], send_sem=ssem.at[g], recv_sem=rsem.at[g],
                                            device_id={"expert": peer(g, c, sign)}, device_id_type=pl.DeviceIdType.MESH)

    def start_group(src, dst, ssem, rsem, g, sign):
        def one(c, carry):
            @pl.when(g + c > 0)
            def _():
                chunk_copy(src, dst, ssem, rsem, g, c, sign).start()
            return carry
        lax.fori_loop(0, nc, one, 0)

    def wait_group(src, dst, ssem, rsem, g, recv):
        def wait(first, count):
            rows = pl.ds(pl.multiple_of(first, WIRE_ROWS), count)
            copy = pltpu.make_async_remote_copy(src_ref=src.at[rows], dst_ref=dst.at[rows], send_sem=ssem.at[g], recv_sem=rsem.at[g],
                                                device_id={"expert": me}, device_id_type=pl.DeviceIdType.MESH)
            copy.wait_recv() if recv else copy.wait_send()

        @pl.when(g == 0)
        def _():
            wait(WIRE_ROWS, wire - WIRE_ROWS)

        @pl.when(g > 0)
        def _():
            wait(g * wire, wire)

    def row_of(ids, slot):
        dz = (ids // (nk * nx * ny) + nz - mz) % nz
        dy = ((ids // (nk * nx)) % ny + ny - my) % ny
        dx = ((ids // nk) % nx + nx - mx) % nx
        dk = (ids % nk + nk - mk) % nk
        return (dx * nk + dk) * dense + slot * nc + dz * ny + dy

    def iota(shape, dim):
        return lax.broadcasted_iota(I32, shape, dim)

    def ones(mask):
        return jnp.where(mask, jnp.float32(1.0), jnp.float32(0.0)).astype(BF16)

    weights_in = pltpu.make_async_copy(win_hbm.at[0], win, w_sem.at[0])
    weights_out = pltpu.make_async_copy(wout_hbm.at[0], wout, w_sem.at[1])
    weights_in.start()
    weights_out.start()

    lanes = iota((tokens, n), 1)
    count = [jnp.sum(jnp.where(ids_col[:, j:j + 1] == lanes, 1, 0).astype(I32), axis=0, keepdims=True) for j in range(2)]
    cbuf[0] = count[0] + count[1] * 65536

    def count_copy(g, c):
        slot = g * nc + c
        return pltpu.make_async_remote_copy(src_ref=cbuf.at[0], dst_ref=cbuf.at[slot], send_sem=c_send.at[0], recv_sem=c_recv.at[0],
                                            device_id={"expert": peer(g, c, 1)}, device_id_type=pl.DeviceIdType.MESH)

    def send_counts(i, carry):
        count_copy(i // nc, i % nc).start()
        return carry
    lax.fori_loop(1, n, send_counts, 0)

    earlier = iota((tokens, tokens), 0) < iota((tokens, tokens), 1)
    row_ids = [ids_row[j:j + 1, :] for j in range(2)]

    def lane_rank(j, other, mask):
        same = ids_col[:, j:j + 1] == row_ids[other]
        if mask:
            same = same & earlier
        return jnp.sum(jnp.where(same, 1, 0).astype(I32), axis=0, keepdims=True)
    rrow[0:1, :] = row_of(row_ids[0], lane_rank(0, 0, True))
    rrow[1:2, :] = row_of(row_ids[1], lane_rank(1, 1, True) + lane_rank(0, 1, False))

    swap = (iota((wire, wire), 0) % WIRE_ROWS) * nc + iota((wire, wire), 0) // WIRE_ROWS
    tmat[...] = ones(swap == iota((wire, wire), 1))
    swap = (iota((wire, wire), 1) % WIRE_ROWS) * nc + iota((wire, wire), 1) // WIRE_ROWS
    tinv[...] = ones(swap == iota((wire, wire), 0))

    step = quarter

    def stack(b, block):
        h, r = (b * quarter) // half, (b * quarter) % half
        st[h * 8 * nc:(h + 1) * 8 * nc, r:r + quarter] = block[:8 * nc]
        st[b * 4 * nc:(b + 1) * 4 * nc, half:half + quarter] = block[8 * nc:12 * nc]
        for o in range(2):
            st[(2 * b + o) * 2 * nc:(2 * b + o + 1) * 2 * nc, half + quarter:width] = block[12 * nc:, o * eighth:(o + 1) * eighth]

    def to_wire(buf, g):
        rows = pl.ds(pl.multiple_of(g * wire, WIRE_ROWS), wire)
        for lo, hi in ((0, quarter), (quarter, half), (half, half + quarter), (half + quarter, width)):
            buf[rows, lo:hi] = jnp.dot(tmat[...], st[:, lo:hi], preferred_element_type=F32).astype(BF16)

    def from_wire(buf, g, dst):
        rows = pl.ds(pl.multiple_of(g * wire, WIRE_ROWS), wire)
        for r in (0, quarter):
            part = jnp.dot(tinv[...], buf[rows, r:r + quarter], preferred_element_type=F32).astype(BF16)
            dst[0:8 * nc, r:r + quarter] = part[:8 * nc]
            dst[0:8 * nc, half + r:half + r + quarter] = part[8 * nc:]
        part = jnp.dot(tinv[...], buf[rows, half:half + quarter], preferred_element_type=F32).astype(BF16)
        for q in range(4):
            dst[8 * nc:12 * nc, q * quarter:(q + 1) * quarter] = part[q * 4 * nc:(q + 1) * 4 * nc]
        part = jnp.dot(tinv[...], buf[rows, half + quarter:width], preferred_element_type=F32).astype(BF16)
        for o in range(8):
            dst[12 * nc:dense, o * eighth:(o + 1) * eighth] = part[o * 2 * nc:(o + 1) * 2 * nc]

    def dispatch(g, carry):
        rows = iota((dense, tokens), 0) + g * dense
        pick = ones((rows == rrow[0:1, :]) | (rows == rrow[1:2, :]))
        for b in range(4):
            block = jnp.dot(pick, x[:, b * step:(b + 1) * step], preferred_element_type=F32).astype(BF16)
            stack(b, block)
        to_wire(outbuf, g)
        start_group(outbuf, inbuf, d_send, d_recv, g, 1)
        return carry
    lax.fori_loop(0, ng, dispatch, 0)
    inbuf[0:WIRE_ROWS, :] = outbuf[0:WIRE_ROWS, :]

    later = iota((tokens, tokens), 1) < iota((tokens, tokens), 0)

    def sub_rank(j, other, mask):
        same = ids_col[:, other:other + 1] == row_ids[j]
        if mask:
            same = same & later
        return jnp.sum(jnp.where(same, 1, 0).astype(I32), axis=1, keepdims=True)
    rank0 = sub_rank(0, 0, True)
    rank1 = sub_rank(1, 1, True)
    rcol[:, 0:1] = row_of(ids_col[:, 0:1], rank0)
    rcol[:, 1:2] = row_of(ids_col[:, 1:2], rank1 + sub_rank(0, 1, False))
    rcol[:, 2:3] = rank0
    rcol[:, 3:4] = rank1

    weights_in.wait()
    weights_out.wait()

    def expert(g, carry):
        wait_group(outbuf, inbuf, d_send, d_recv, g, True)
        from_wire(inbuf, g, xs)
        for b in range(4):
            cols = slice(b * hidden // 4, (b + 1) * hidden // 4)
            pre = jnp.dot(xs[0:dense, :], win[:, cols], preferred_element_type=F32)
            hs[:, cols] = jax.nn.gelu(pre).astype(BF16)
        for b in range(4):
            block = jnp.dot(hs[...], wout[:, b * step:(b + 1) * step], preferred_element_type=F32).astype(BF16)
            stack(b, block)
        to_wire(obuf, g)
        start_group(obuf, retbuf, r_send, r_recv, g, -1)
        return carry
    lax.fori_loop(0, ng, expert, 0)
    retbuf[0:WIRE_ROWS, :] = obuf[0:WIRE_ROWS, :]

    pltpu.make_async_remote_copy(src_ref=cbuf.at[pl.ds(1, n - 1)], dst_ref=cbuf.at[pl.ds(1, n - 1)], send_sem=c_send.at[0], recv_sem=c_recv.at[0],
                                 device_id={"expert": me}, device_id_type=pl.DeviceIdType.MESH).wait()

    def add_counts(i, carry):
        before0, before1, total0 = carry
        packed = cbuf[i]
        second = packed // 65536
        first = packed - second * 65536
        use = jnp.where(peer(i // nc, i % nc, -1) < me, 1, 0).astype(I32)
        return before0 + first * use, before1 + second * use, total0 + first
    zero = jnp.zeros((1, n), I32)
    before0, before1, total0 = lax.fori_loop(0, n, add_counts, (zero, zero, zero))
    for j, offset in enumerate((before0, total0 + before1)):
        mine = jnp.sum(jnp.where(ids_col[:, j:j + 1] == lanes, offset, 0), axis=1, keepdims=True)
        wcol[:, j:j + 1] = jnp.where(mine + rcol[:, 2 + j:3 + j] < capacity, gates[:, j:j + 1], 0.0)

    acc0[...] = jnp.zeros_like(acc0)
    acc1[...] = jnp.zeros_like(acc1)
    xs[dense:wire, :] = jnp.zeros((wire - dense, model), BF16)

    def combine(g, carry):
        wait_group(obuf, retbuf, r_send, r_recv, g, True)
        from_wire(retbuf, g, xs)
        cols = iota((tokens, wire), 1)
        for j, acc in enumerate((acc0, acc1)):
            want = rcol[:, j:j + 1] - g * dense
            pick = ones((want == cols) & (cols < dense))
            for b in range(4):
                part = slice(b * step, (b + 1) * step)
                acc[:, part] += jnp.dot(pick, xs[:, part], preferred_element_type=F32)
        return carry
    lax.fori_loop(0, ng, combine, 0)
    out[...] = (x[...].astype(F32) + wcol[:, 0:1] * acc0[...] + wcol[:, 1:2] * acc1[...]).astype(BF16)

    def drain(g, carry):
        wait_group(outbuf, inbuf, d_send, d_recv, g, False)
        wait_group(obuf, retbuf, r_send, r_recv, g, False)
        return carry
    lax.fori_loop(0, ng, drain, 0)


def torus(n):
    return (4, 4, 4, 2) if n == 128 else (2, n // 4, 1, 2)


def solution(mesh):
    n = mesh.shape["expert"]
    row_spec = P(("data", "expert"), None)
    weight_spec = P("expert", None, None)
    dims = torus(n)

    def device_step(token_rows, expert_ids, gate_weights, w_in, w_out):
        tokens, model = token_rows.shape
        hidden = w_in.shape[2]
        nc, ng = dims[0] * dims[1], dims[2] * dims[3]
        wire, dense = nc * WIRE_ROWS, nc * SLOTS
        width = SLOTS * model // WIRE_ROWS
        capacity = n * (tokens * 2 // n)
        vmem = pl.BlockSpec(memory_space=pltpu.VMEM)
        hbm = pl.BlockSpec(memory_space=pl.ANY)
        dma = pltpu.SemaphoreType.DMA
        return pl.pallas_call(
            functools.partial(moe_kernel, dims, capacity),
            out_shape=jax.ShapeDtypeStruct((tokens, model), BF16),
            in_specs=[vmem, vmem, vmem, vmem, hbm, hbm],
            out_specs=vmem,
            scratch_shapes=[
                pltpu.VMEM((ng * wire, width), BF16),
                pltpu.VMEM((ng * wire, width), BF16),
                pltpu.VMEM((ng * wire, width), BF16),
                pltpu.VMEM((ng * wire, width), BF16),
                pltpu.VMEM((n, 1, n), I32),
                pltpu.VMEM((model, hidden), BF16),
                pltpu.VMEM((hidden, model), BF16),
                pltpu.VMEM((wire, width), BF16),
                pltpu.VMEM((wire, model), BF16),
                pltpu.VMEM((dense, hidden), BF16),
                pltpu.VMEM((tokens, model), F32),
                pltpu.VMEM((tokens, model), F32),
                pltpu.VMEM((wire, wire), BF16),
                pltpu.VMEM((wire, wire), BF16),
                pltpu.VMEM((2, tokens), I32),
                pltpu.VMEM((tokens, 4), I32),
                pltpu.VMEM((tokens, 2), F32),
                dma((2,)), dma((1,)), dma((1,)), dma((ng,)), dma((ng,)), dma((ng,)), dma((ng,)),
            ],
            compiler_params=pltpu.CompilerParams(has_side_effects=True, vmem_limit_bytes=60 * 1024 * 1024),
        )(expert_ids.T, expert_ids, gate_weights, token_rows, w_in, w_out)

    return jax.shard_map(device_step, mesh=mesh, in_specs=(row_spec, row_spec, row_spec, weight_spec, weight_spec), out_specs=row_spec, check_vma=False)
```

time: 330 us -> 145 us (0.44)
  the two profiles are of different devices: /device:TPU:0 before, /device:TPU:7 now
where the time goes in v1:
time: 145 us
  Pallas kernels  140 us (97%)
  local copies, waits for them, and re-layouts  5.36 us (4%)
    pallas_call x1, Pallas kernels, device_step(): pl.pallas_call(functools.partial(moe_kernel, dims, capacity), out_shape=j...  140 us
    unnamed x3, local copies, waits for them, and re-layouts  5.36 us

profile of v1, /device:TPU:7, one launch (start us, length us, event | category | flops | bytes accessed | tf_op | source)
XLA Modules:
  0.0 144.9 jit_solution(16825648338916444491)
XLA Ops:
  0.0 1.6 %copy.7.gates = f32[512,2]{1,0:T(8,128)} copy(f32[512,2]{0,1:T(2,128)} %param.7) | data formatting | bytes 8192 | tf_op args[2]
  1.6 1.5 %copy.6.ids_col = s32[512,2]{1,0:T(8,128)} copy(s32[512,2]{0,1:T(2,128)} %param.6) | data formatting | bytes 8192 | tf_op args[1]
  3.1 139.5 %shard_map.55 = bf16[512,1024]{1,0:T(8,128)(2,1)} custom-call(s32[2,512]{1,0:T(2,128)} %bitcast.1, s32[512,2]{1,0:T(8,128)} %copy.6.ids_col, f32[512,2]{1,0:T(8,128)} %copy.7.gates, bf16[512,1024]{1,0:T(8,128)(2,1)} %x.1, bf16[1,1024,1024]{2,1,0:T(8,128)(2,1)} %win_hbm.1, bf16[1,1024,1024]{2,1,0:T(8,128)(2,1)} %wout_hbm.1), custom_call_target="tpu_custom_call" | custom-call | tf_op jit(solution)/shard_map/pallas_call | solution.py:252
  142.6 2.3 %copy.9 = bf16[512,1024]{1,0:T(8,128)(2,1)} copy(bf16[512,1024]{1,0:T(8,128)(2,1)} %shard_map.55) | data formatting | bytes 2097152

commit v2 on v1

--- a/solution.py
+++ b/solution.py
@@ -14,8 +14,8 @@
 I32 = jnp.int32
 
 
-def moe_kernel(dims, capacity, ids_row, ids_col, gates, x, win_hbm, wout_hbm, out,
-               outbuf, inbuf, obuf, retbuf, cbuf, win, wout, st, xs, hs, acc0, acc1, tmat, tinv, rrow, rcol, wcol,
+def moe_kernel(dims, capacity, ids_row, gates_row, x, win_hbm, wout_hbm, out,
+               outbuf, inbuf, obuf, retbuf, cbuf, win, wout, st, xs, hs, acc0, acc1, tmat, tinv, rrow, rcol, wcol, flat, turned,
                w_sem, c_send, c_recv, d_send, d_recv, r_send, r_recv):
     nz, ny, nx, nk = dims
     n = nz * ny * nx * nk
@@ -27,31 +27,38 @@
     half, quarter, eighth = model // 2, model // 4, model // 8
     width = SLOTS * model // WIRE_ROWS
     me = lax.axis_index("expert")
-    mk = me % nk
-    mx = (me // nk) % nx
-    my = (me // (nk * nx)) % ny
-    mz = me // (nk * nx * ny)
-
-    def peer(g, c, sign):
-        dx, dk, dz, dy = g // nk, g % nk, c // ny, c % ny
-        z = (mz + nz + sign * dz) % nz
-        y = (my + ny + sign * dy) % ny
-        xx = (mx + nx + sign * dx) % nx
-        k = (mk + nk + sign * dk) % nk
-        return ((z * ny + y) * nx + xx) * nk + k
-
-    def chunk_copy(src, dst, ssem, rsem, g, c, sign):
-        rows = pl.ds(pl.multiple_of(g * wire + c * WIRE_ROWS, WIRE_ROWS), WIRE_ROWS)
-        return pltpu.make_async_remote_copy(src_ref=src.at[rows], dst_ref=dst.at[rows], send_sem=ssem.at[g], recv_sem=rsem.at[g],
-                                            device_id={"expert": peer(g, c, sign)}, device_id_type=pl.DeviceIdType.MESH)
+    mk = lax.rem(me, nk)
+    mx = lax.rem(lax.div(me, nk), nx)
+    my = lax.rem(lax.div(me, nk * nx), ny)
+    mz = lax.div(me, nk * nx * ny)
+
+    def digits(sign):
+        zs = [lax.rem(mz + nz + sign * d, nz) * (ny * nx * nk) for d in range(nz)]
+        ys = [lax.rem(my + ny + sign * d, ny) * (nx * nk) for d in range(ny)]
+        return [zs[c // ny] + ys[c % ny] for c in range(nc)]
+    ahead, behind = digits(1), digits(-1)
+
+    def base_of(g, sign):
+        dx, dk = lax.div(g, nk), lax.rem(g, nk)
+        return lax.rem(mx + nx + sign * dx, nx) * nk + lax.rem(mk + nk + sign * dk, nk)
+
+    def each_peer(g, sign, act):
+        base = base_of(g, sign)
+        for c in range(nc):
+            device = (ahead if sign > 0 else behind)[c] + base
+            if c > 0:
+                act(c, device)
+            else:
+                @pl.when(g > 0)
+                def _():
+                    act(c, device)
 
     def start_group(src, dst, ssem, rsem, g, sign):
-        def one(c, carry):
-            @pl.when(g + c > 0)
-            def _():
-                chunk_copy(src, dst, ssem, rsem, g, c, sign).start()
-            return carry
-        lax.fori_loop(0, nc, one, 0)
+        def act(c, device):
+            rows = pl.ds(pl.multiple_of(g * wire + c * WIRE_ROWS, WIRE_ROWS), WIRE_ROWS)
+            pltpu.make_async_remote_copy(src_ref=src.at[rows], dst_ref=dst.at[rows], send_sem=ssem.at[g], recv_sem=rsem.at[g],
+                                         device_id={"expert": device}, device_id_type=pl.DeviceIdType.MESH).start()
+        each_peer(g, sign, act)
 
     def wait_group(src, dst, ssem, rsem, g, recv):
         def wait(first, count):
@@ -81,24 +88,25 @@
     def ones(mask):
         return jnp.where(mask, jnp.float32(1.0), jnp.float32(0.0)).astype(BF16)
 
+    barrier = pltpu.get_barrier_semaphore()
+
+    def hello(g, carry):
+        def act(c, device):
+            pl.semaphore_signal(barrier, inc=1, device_id={"expert": device}, device_id_type=pl.DeviceIdType.MESH)
+        each_peer(g, 1, act)
+        return carry
+    lax.fori_loop(0, ng, hello, 0)
+
     weights_in = pltpu.make_async_copy(win_hbm.at[0], win, w_sem.at[0])
     weights_out = pltpu.make_async_copy(wout_hbm.at[0], wout, w_sem.at[1])
     weights_in.start()
     weights_out.start()
 
-    lanes = iota((tokens, n), 1)
-    count = [jnp.sum(jnp.where(ids_col[:, j:j + 1] == lanes, 1, 0).astype(I32), axis=0, keepdims=True) for j in range(2)]
-    cbuf[0] = count[0] + count[1] * 65536
-
-    def count_copy(g, c):
-        slot = g * nc + c
-        return pltpu.make_async_remote_copy(src_ref=cbuf.at[0], dst_ref=cbuf.at[slot], send_sem=c_send.at[0], recv_sem=c_recv.at[0],
-                                            device_id={"expert": peer(g, c, 1)}, device_id_type=pl.DeviceIdType.MESH)
-
-    def send_counts(i, carry):
-        count_copy(i // nc, i % nc).start()
-        return carry
-    lax.fori_loop(1, n, send_counts, 0)
+    flat[0:2, :] = ids_row[...].astype(F32)
+    flat[2:4, :] = gates_row[...]
+    flat[4:8, :] = jnp.zeros((4, tokens), F32)
+    turned[...] = flat[...].T
+    ids_col = turned[:, 0:2].astype(I32)
 
     earlier = iota((tokens, tokens), 0) < iota((tokens, tokens), 1)
     row_ids = [ids_row[j:j + 1, :] for j in range(2)]
@@ -143,16 +151,34 @@
         for o in range(8):
             dst[12 * nc:dense, o * eighth:(o + 1) * eighth] = part[o * 2 * nc:(o + 1) * 2 * nc]
 
-    def dispatch(g, carry):
+    def build(g, carry):
         rows = iota((dense, tokens), 0) + g * dense
         pick = ones((rows == rrow[0:1, :]) | (rows == rrow[1:2, :]))
         for b in range(4):
             block = jnp.dot(pick, x[:, b * step:(b + 1) * step], preferred_element_type=F32).astype(BF16)
             stack(b, block)
         to_wire(outbuf, g)
+        return carry
+    lax.fori_loop(0, ng, build, 0)
+
+    lanes = iota((tokens, n), 1)
+    count = [jnp.sum(jnp.where(ids_col[:, j:j + 1] == lanes, 1, 0).astype(I32), axis=0, keepdims=True) for j in range(2)]
+    cbuf[0] = count[0] + count[1] * 65536
+
+    pl.semaphore_wait(barrier, n - 1)
+
+    def dispatch(g, carry):
         start_group(outbuf, inbuf, d_send, d_recv, g, 1)
         return carry
     lax.fori_loop(0, ng, dispatch, 0)
+
+    def send_counts(g, carry):
+        def act(c, device):
+            pltpu.make_async_remote_copy(src_ref=cbuf.at[0], dst_ref=cbuf.at[g * nc + c], send_sem=c_send.at[0], recv_sem=c_recv.at[0],
+                                         device_id={"expert": device}, device_id_type=pl.DeviceIdType.MESH).start()
+        each_peer(g, 1, act)
+        return carry
+    lax.fori_loop(0, ng, send_counts, 0)
     inbuf[0:WIRE_ROWS, :] = outbuf[0:WIRE_ROWS, :]
 
     later = iota((tokens, tokens), 1) < iota((tokens, tokens), 0)
@@ -191,18 +217,18 @@
     pltpu.make_async_remote_copy(src_ref=cbuf.at[pl.ds(1, n - 1)], dst_ref=cbuf.at[pl.ds(1, n - 1)], send_sem=c_send.at[0], recv_sem=c_recv.at[0],
                                  device_id={"expert": me}, device_id_type=pl.DeviceIdType.MESH).wait()
 
-    def add_counts(i, carry):
-        before0, before1, total0 = carry
-        packed = cbuf[i]
-        second = packed // 65536
-        first = packed - second * 65536
-        use = jnp.where(peer(i // nc, i % nc, -1) < me, 1, 0).astype(I32)
-        return before0 + first * use, before1 + second * use, total0 + first
-    zero = jnp.zeros((1, n), I32)
-    before0, before1, total0 = lax.fori_loop(0, n, add_counts, (zero, zero, zero))
+    packed = cbuf[...].reshape(n, n)
+    second = packed // 65536
+    first = packed - second * 65536
+    slot = iota((n, n), 0)
+    dx, dk, dz, dy = (slot // nc) // nk, (slot // nc) % nk, (slot % nc) // ny, (slot % nc) % ny
+    source = (((mz + nz - dz) % nz * ny + (my + ny - dy) % ny) * nx + (mx + nx - dx) % nx) * nk + (mk + nk - dk) % nk
+    before0 = jnp.sum(jnp.where(source < me, first, 0), axis=0, keepdims=True)
+    before1 = jnp.sum(jnp.where(source < me, second, 0), axis=0, keepdims=True)
+    total0 = jnp.sum(first, axis=0, keepdims=True)
     for j, offset in enumerate((before0, total0 + before1)):
         mine = jnp.sum(jnp.where(ids_col[:, j:j + 1] == lanes, offset, 0), axis=1, keepdims=True)
-        wcol[:, j:j + 1] = jnp.where(mine + rcol[:, 2 + j:3 + j] < capacity, gates[:, j:j + 1], 0.0)
+        wcol[:, j:j + 1] = jnp.where(mine + rcol[:, 2 + j:3 + j] < capacity, turned[:, 2 + j:3 + j], 0.0)
 
     acc0[...] = jnp.zeros_like(acc0)
     acc1[...] = jnp.zeros_like(acc1)
@@ -252,7 +278,7 @@
         return pl.pallas_call(
             functools.partial(moe_kernel, dims, capacity),
             out_shape=jax.ShapeDtypeStruct((tokens, model), BF16),
-            in_specs=[vmem, vmem, vmem, vmem, hbm, hbm],
+            in_specs=[vmem, vmem, vmem, hbm, hbm],
             out_specs=vmem,
             scratch_shapes=[
                 pltpu.VMEM((ng * wire, width), BF16),
@@ -272,9 +298,11 @@
                 pltpu.VMEM((2, tokens), I32),
                 pltpu.VMEM((tokens, 4), I32),
                 pltpu.VMEM((tokens, 2), F32),
+                pltpu.VMEM((8, tokens), F32),
+                pltpu.VMEM((tokens, 8), F32),
                 dma((2,)), dma((1,)), dma((1,)), dma((ng,)), dma((ng,)), dma((ng,)), dma((ng,)),
             ],
-            compiler_params=pltpu.CompilerParams(has_side_effects=True, vmem_limit_bytes=60 * 1024 * 1024),
-        )(expert_ids.T, expert_ids, gate_weights, token_rows, w_in, w_out)
+            compiler_params=pltpu.CompilerParams(has_side_effects=True, collective_id=0, vmem_limit_bytes=60 * 1024 * 1024),
+        )(expert_ids.T, gate_weights.T, token_rows, w_in, w_out)
 
     return jax.shard_map(device_step, mesh=mesh, in_specs=(row_spec, row_spec, row_spec, weight_spec, weight_spec), out_specs=row_spec, check_vma=False)

time: 145 us -> 122 us (0.84)
  the two profiles are of different devices: /device:TPU:7 before, /device:TPU:6 now
where the time goes in v2:
time: 122 us
  Pallas kernels  120 us (98%)
  local copies, waits for them, and re-layouts  2.26 us (2%)
    pallas_call x1, Pallas kernels, device_step(): pl.pallas_call(functools.partial(moe_kernel, dims, capacity), out_shape=j...  120 us

profile of v2, /device:TPU:6, one launch (start us, length us, event | category | flops | bytes accessed | tf_op | source)
XLA Modules:
  0.0 122.1 jit_solution(4517387513877431423)
XLA Ops:
  0.0 119.8 %shard_map.55 = bf16[512,1024]{1,0:T(8,128)(2,1)} custom-call(s32[2,512]{1,0:T(2,128)} %bitcast.2, f32[2,512]{1,0:T(2,128)} %bitcast.3, bf16[512,1024]{1,0:T(8,128)(2,1)} %x.1, bf16[1,1024,1024]{2,1,0:T(8,128)(2,1)} %win_hbm.1, bf16[1,1024,1024]{2,1,0:T(8,128)(2,1)} %wout_hbm.1), custom_call_target="tpu_custom_call" | custom-call | tf_op jit(solution)/shard_map/pallas_call | solution.py:278
  119.8 2.3 %copy.7 = bf16[512,1024]{1,0:T(8,128)(2,1)} copy(bf16[512,1024]{1,0:T(8,128)(2,1)} %shard_map.55) | data formatting | bytes 2097152

commit v3 on v2

--- a/solution.py
+++ b/solution.py
@@ -12,6 +12,7 @@
 BF16 = jnp.bfloat16
 F32 = jnp.float32
 I32 = jnp.int32
+XORDER = {4: (1, 3, 2, 0), 2: (1, 0)}
 
 
 def moe_kernel(dims, capacity, ids_row, gates_row, x, win_hbm, wout_hbm, out,
@@ -32,26 +33,32 @@
     my = lax.rem(lax.div(me, nk * nx), ny)
     mz = lax.div(me, nk * nx * ny)
 
-    def digits(sign):
-        zs = [lax.rem(mz + nz + sign * d, nz) * (ny * nx * nk) for d in range(nz)]
-        ys = [lax.rem(my + ny + sign * d, ny) * (nx * nk) for d in range(ny)]
-        return [zs[c // ny] + ys[c % ny] for c in range(nc)]
-    ahead, behind = digits(1), digits(-1)
-
-    def base_of(g, sign):
-        dx, dk = lax.div(g, nk), lax.rem(g, nk)
-        return lax.rem(mx + nx + sign * dx, nx) * nk + lax.rem(mk + nk + sign * dk, nk)
+    half_z, half_y = nz // 2, ny // 2
+    turn = XORDER[nx]
 
     def each_peer(g, sign, act):
-        base = base_of(g, sign)
+        u, rk = lax.div(g, nk), lax.rem(g, nk)
+        core = mk if sign > 0 else lax.rem(mk + rk, nk)
+        base = lax.rem(mk + rk, nk)
+        parts = {}
         for c in range(nc):
-            device = (ahead if sign > 0 else behind)[c] + base
-            if c > 0:
-                act(c, device)
-            else:
-                @pl.when(g > 0)
+            i, dx = c // nx, turn[c % nx]
+            mirror = -1 if 2 * dx > nx else 1
+            if (i, mirror) not in parts:
+                dz = lax.rem(nz + mirror * i + core * half_z, nz)
+                dy = lax.rem(2 * ny + mirror * (u + i) + core * half_y, ny)
+                z = lax.rem(mz + nz + sign * dz, nz)
+                y = lax.rem(my + ny + sign * dy, ny)
+                parts[i, mirror] = (z * ny + y) * (nx * nk) + base
+            device = parts[i, mirror] + lax.rem(mx + nx + sign * dx, nx) * nk
+            if dx == 0:
+                @pl.when(device != me)
                 def _():
                     act(c, device)
+            else:
+                act(c, device)
+    own = (mk * half_z) * nx + turn.index(0)
+    own_rows = pl.ds(pl.multiple_of(own * WIRE_ROWS, WIRE_ROWS), WIRE_ROWS)
 
     def start_group(src, dst, ssem, rsem, g, sign):
         def act(c, device):
@@ -76,11 +83,15 @@
             wait(g * wire, wire)
 
     def row_of(ids, slot):
-        dz = (ids // (nk * nx * ny) + nz - mz) % nz
-        dy = ((ids // (nk * nx)) % ny + ny - my) % ny
+        dz = (ids // (nk * nx * ny) + nz - mz + mk * half_z) % nz
+        dy = ((ids // (nk * nx)) % ny + ny - my + mk * half_y) % ny
         dx = ((ids // nk) % nx + nx - mx) % nx
         dk = (ids % nk + nk - mk) % nk
-        return (dx * nk + dk) * dense + slot * nc + dz * ny + dy
+        flip = 2 * dx > nx
+        i = jnp.where(flip, (nz - dz) % nz, dz)
+        u = (jnp.where(flip, (ny - dy) % ny, dy) + ny - i) % ny
+        q = sum(jnp.where(dx == d, p, 0) for p, d in enumerate(turn))
+        return (u * nk + dk) * dense + slot * nc + i * nx + q
 
     def iota(shape, dim):
         return lax.broadcasted_iota(I32, shape, dim)
@@ -163,7 +174,7 @@
 
     lanes = iota((tokens, n), 1)
     count = [jnp.sum(jnp.where(ids_col[:, j:j + 1] == lanes, 1, 0).astype(I32), axis=0, keepdims=True) for j in range(2)]
-    cbuf[0] = count[0] + count[1] * 65536
+    cbuf[own] = count[0] + count[1] * 65536
 
     pl.semaphore_wait(barrier, n - 1)
 
@@ -174,12 +185,12 @@
 
     def send_counts(g, carry):
         def act(c, device):
-            pltpu.make_async_remote_copy(src_ref=cbuf.at[0], dst_ref=cbuf.at[g * nc + c], send_sem=c_send.at[0], recv_sem=c_recv.at[0],
+            pltpu.make_async_remote_copy(src_ref=cbuf.at[own], dst_ref=cbuf.at[g * nc + c], send_sem=c_send.at[0], recv_sem=c_recv.at[0],
                                          device_id={"expert": device}, device_id_type=pl.DeviceIdType.MESH).start()
         each_peer(g, 1, act)
         return carry
     lax.fori_loop(0, ng, send_counts, 0)
-    inbuf[0:WIRE_ROWS, :] = outbuf[0:WIRE_ROWS, :]
+    inbuf[own_rows, :] = outbuf[own_rows, :]
 
     later = iota((tokens, tokens), 1) < iota((tokens, tokens), 0)
 
@@ -212,7 +223,7 @@
         start_group(obuf, retbuf, r_send, r_recv, g, -1)
         return carry
     lax.fori_loop(0, ng, expert, 0)
-    retbuf[0:WIRE_ROWS, :] = obuf[0:WIRE_ROWS, :]
+    retbuf[own_rows, :] = obuf[own_rows, :]
 
     pltpu.make_async_remote_copy(src_ref=cbuf.at[pl.ds(1, n - 1)], dst_ref=cbuf.at[pl.ds(1, n - 1)], send_sem=c_send.at[0], recv_sem=c_recv.at[0],
                                  device_id={"expert": me}, device_id_type=pl.DeviceIdType.MESH).wait()
@@ -221,8 +232,14 @@
     second = packed // 65536
     first = packed - second * 65536
     slot = iota((n, n), 0)
-    dx, dk, dz, dy = (slot // nc) // nk, (slot // nc) % nk, (slot % nc) // ny, (slot % nc) % ny
-    source = (((mz + nz - dz) % nz * ny + (my + ny - dy) % ny) * nx + (mx + nx - dx) % nx) * nk + (mk + nk - dk) % nk
+    g, c = slot // nc, slot % nc
+    u, rk, i = g // nk, g % nk, c // nx
+    dx = sum(jnp.where(c % nx == p, d, 0) for p, d in enumerate(turn))
+    mirror = jnp.where(2 * dx > nx, -1, 1)
+    core = (mk + rk) % nk
+    dz = (nz + mirror * i + core * half_z) % nz
+    dy = (2 * ny + mirror * (u + i) + core * half_y) % ny
+    source = (((mz + nz - dz) % nz * ny + (my + ny - dy) % ny) * nx + (mx + nx - dx) % nx) * nk + core
     before0 = jnp.sum(jnp.where(source < me, first, 0), axis=0, keepdims=True)
     before1 = jnp.sum(jnp.where(source < me, second, 0), axis=0, keepdims=True)
     total0 = jnp.sum(first, axis=0, keepdims=True)
@@ -256,7 +273,7 @@
 
 
 def torus(n):
-    return (4, 4, 4, 2) if n == 128 else (2, n // 4, 1, 2)
+    return (4, 4, 4, 2) if n == 128 else (2, 2, 2, 2)
 
 
 def solution(mesh):

time: 122 us -> 119 us (0.975)
  the two profiles are of different devices: /device:TPU:6 before, /device:TPU:30 now
where the time goes in v3:
time: 119 us
  Pallas kernels  117 us (98%)
  local copies, waits for them, and re-layouts  2.26 us (2%)
    pallas_call x1, Pallas kernels, device_step(): pl.pallas_call(functools.partial(moe_kernel, dims, capacity), out_shape=j...  117 us

profile of v3, /device:TPU:30, one launch (start us, length us, event | category | flops | bytes accessed | tf_op | source)
XLA Modules:
  0.0 119.2 jit_solution(16706291953732994098)
XLA Ops:
  0.0 117.0 %shard_map.55 = bf16[512,1024]{1,0:T(8,128)(2,1)} custom-call(s32[2,512]{1,0:T(2,128)} %bitcast.2, f32[2,512]{1,0:T(2,128)} %bitcast.3, bf16[512,1024]{1,0:T(8,128)(2,1)} %x.1, bf16[1,1024,1024]{2,1,0:T(8,128)(2,1)} %win_hbm.1, bf16[1,1024,1024]{2,1,0:T(8,128)(2,1)} %wout_hbm.1), custom_call_target="tpu_custom_call" | custom-call | tf_op jit(solution)/shard_map/pallas_call | solution.py:295
  117.0 2.3 %copy.7 = bf16[512,1024]{1,0:T(8,128)(2,1)} copy(bf16[512,1024]{1,0:T(8,128)(2,1)} %shard_map.55) | data formatting | bytes 2097152

commit v4 on v3

--- a/solution.py
+++ b/solution.py
@@ -12,16 +12,17 @@
 BF16 = jnp.bfloat16
 F32 = jnp.float32
 I32 = jnp.int32
+VMEM_LIMIT = 60 * 1024 * 1024
 XORDER = {4: (1, 3, 2, 0), 2: (1, 0)}
 
 
-def moe_kernel(dims, capacity, ids_row, gates_row, x, win_hbm, wout_hbm, out,
-               outbuf, inbuf, obuf, retbuf, cbuf, win, wout, st, xs, hs, acc0, acc1, tmat, tinv, rrow, rcol, wcol, flat, turned,
+def moe_kernel(dims, capacity, ids_hbm, gates_hbm, x_hbm, win_hbm, wout_hbm, out,
+               ids_row, gates_row, x, outbuf, inbuf, obuf, retbuf, cbuf, win, wout, st, xs, hs, acc0, acc1, tmat, tinv, rrow, rcol, wcol, flat, turned,
                w_sem, c_send, c_recv, d_send, d_recv, r_send, r_recv):
     nz, ny, nx, nk = dims
     n = nz * ny * nx * nk
     nc, ng = nz * ny, nx * nk
-    tokens, model = x.shape
+    tokens, model = x_hbm.shape
     hidden = win.shape[1]
     dense = SLOTS * nc
     wire = WIRE_ROWS * nc
@@ -99,19 +100,19 @@
     def ones(mask):
         return jnp.where(mask, jnp.float32(1.0), jnp.float32(0.0)).astype(BF16)
 
+    fetch = [pltpu.make_async_copy(src, dst, w_sem.at[i]) for i, (src, dst) in enumerate((
+        (ids_hbm, ids_row), (gates_hbm, gates_row), (x_hbm, x), (win_hbm.at[0], win), (wout_hbm.at[0], wout)))]
+    for copy in fetch:
+        copy.start()
+
     barrier = pltpu.get_barrier_semaphore()
 
-    def hello(g, carry):
-        def act(c, device):
-            pl.semaphore_signal(barrier, inc=1, device_id={"expert": device}, device_id_type=pl.DeviceIdType.MESH)
-        each_peer(g, 1, act)
-        return carry
-    lax.fori_loop(0, ng, hello, 0)
-
-    weights_in = pltpu.make_async_copy(win_hbm.at[0], win, w_sem.at[0])
-    weights_out = pltpu.make_async_copy(wout_hbm.at[0], wout, w_sem.at[1])
-    weights_in.start()
-    weights_out.start()
+    def hello(i, carry):
+        pl.semaphore_signal(barrier, inc=1, device_id={"expert": lax.rem(me + i, n)}, device_id_type=pl.DeviceIdType.MESH)
+        return carry
+    lax.fori_loop(1, n, hello, 0, unroll=4)
+    fetch[0].wait()
+    fetch[1].wait()
 
     flat[0:2, :] = ids_row[...].astype(F32)
     flat[2:4, :] = gates_row[...]
@@ -170,7 +171,8 @@
             stack(b, block)
         to_wire(outbuf, g)
         return carry
-    lax.fori_loop(0, ng, build, 0)
+    fetch[2].wait()
+    lax.fori_loop(0, ng // 2, build, 0)
 
     lanes = iota((tokens, n), 1)
     count = [jnp.sum(jnp.where(ids_col[:, j:j + 1] == lanes, 1, 0).astype(I32), axis=0, keepdims=True) for j in range(2)]
@@ -181,7 +183,11 @@
     def dispatch(g, carry):
         start_group(outbuf, inbuf, d_send, d_recv, g, 1)
         return carry
-    lax.fori_loop(0, ng, dispatch, 0)
+    lax.fori_loop(0, ng // 2, dispatch, 0)
+
+    def build_dispatch(g, carry):
+        return dispatch(g, build(g, carry))
+    lax.fori_loop(ng // 2, ng, build_dispatch, 0)
 
     def send_counts(g, carry):
         def act(c, device):
@@ -206,8 +212,8 @@
     rcol[:, 2:3] = rank0
     rcol[:, 3:4] = rank1
 
-    weights_in.wait()
-    weights_out.wait()
+    fetch[3].wait()
+    fetch[4].wait()
 
     def expert(g, carry):
         wait_group(outbuf, inbuf, d_send, d_recv, g, True)
@@ -251,19 +257,30 @@
     acc1[...] = jnp.zeros_like(acc1)
     xs[dense:wire, :] = jnp.zeros((wire - dense, model), BF16)
 
+    def picks(g):
+        cols = iota((tokens, wire), 1)
+        wants = [rcol[:, j:j + 1] - g * dense for j in range(2)]
+        return [ones((want == cols) & (cols < dense)) for want in wants]
+
     def combine(g, carry):
         wait_group(obuf, retbuf, r_send, r_recv, g, True)
         from_wire(retbuf, g, xs)
-        cols = iota((tokens, wire), 1)
-        for j, acc in enumerate((acc0, acc1)):
-            want = rcol[:, j:j + 1] - g * dense
-            pick = ones((want == cols) & (cols < dense))
+        for pick, acc in zip(picks(g), (acc0, acc1)):
             for b in range(4):
                 part = slice(b * step, (b + 1) * step)
                 acc[:, part] += jnp.dot(pick, xs[:, part], preferred_element_type=F32)
         return carry
-    lax.fori_loop(0, ng, combine, 0)
-    out[...] = (x[...].astype(F32) + wcol[:, 0:1] * acc0[...] + wcol[:, 1:2] * acc1[...]).astype(BF16)
+    lax.fori_loop(0, ng - 1, combine, 0)
+
+    last = ng - 1
+    wait_group(obuf, retbuf, r_send, r_recv, last, True)
+    from_wire(retbuf, last, xs)
+    pick0, pick1 = picks(last)
+    for b in range(4):
+        part = slice(b * step, (b + 1) * step)
+        first = acc0[:, part] + jnp.dot(pick0, xs[:, part], preferred_element_type=F32)
+        second = acc1[:, part] + jnp.dot(pick1, xs[:, part], preferred_element_type=F32)
+        out[:, part] = (x[:, part].astype(F32) + wcol[:, 0:1] * first + wcol[:, 1:2] * second).astype(BF16)
 
     def drain(g, carry):
         wait_group(outbuf, inbuf, d_send, d_recv, g, False)
@@ -290,14 +307,17 @@
         width = SLOTS * model // WIRE_ROWS
         capacity = n * (tokens * 2 // n)
         vmem = pl.BlockSpec(memory_space=pltpu.VMEM)
-        hbm = pl.BlockSpec(memory_space=pl.ANY)
+        hbm = pl.BlockSpec(memory_space=pltpu.HBM)
         dma = pltpu.SemaphoreType.DMA
         return pl.pallas_call(
             functools.partial(moe_kernel, dims, capacity),
             out_shape=jax.ShapeDtypeStruct((tokens, model), BF16),
-            in_specs=[vmem, vmem, vmem, hbm, hbm],
+            in_specs=[hbm] * 5,
             out_specs=vmem,
             scratch_shapes=[
+                pltpu.VMEM((2, tokens), I32),
+                pltpu.VMEM((2, tokens), F32),
+                pltpu.VMEM((tokens, model), BF16),
                 pltpu.VMEM((ng * wire, width), BF16),
                 pltpu.VMEM((ng * wire, width), BF16),
                 pltpu.VMEM((ng * wire, width), BF16),
@@ -317,9 +337,9 @@
                 pltpu.VMEM((tokens, 2), F32),
                 pltpu.VMEM((8, tokens), F32),
                 pltpu.VMEM((tokens, 8), F32),
-                dma((2,)), dma((1,)), dma((1,)), dma((ng,)), dma((ng,)), dma((ng,)), dma((ng,)),
+                dma((5,)), dma((1,)), dma((1,)), dma((ng,)), dma((ng,)), dma((ng,)), dma((ng,)),
             ],
-            compiler_params=pltpu.CompilerParams(has_side_effects=True, collective_id=0, vmem_limit_bytes=60 * 1024 * 1024),
+            compiler_params=pltpu.CompilerParams(has_side_effects=True, collective_id=0, vmem_limit_bytes=VMEM_LIMIT),
         )(expert_ids.T, gate_weights.T, token_rows, w_in, w_out)
 
     return jax.shard_map(device_step, mesh=mesh, in_specs=(row_spec, row_spec, row_spec, weight_spec, weight_spec), out_specs=row_spec, check_vma=False)

time: 119 us -> 114 us (0.958)
  the two profiles are of different devices: /device:TPU:30 before, /device:TPU:1 now
where the time goes in v4:
time: 114 us
  Pallas kernels  112 us (98%)
  local copies, waits for them, and re-layouts  2.26 us (2%)
    pallas_call x1, Pallas kernels, device_step(): pl.pallas_call(functools.partial(moe_kernel, dims, capacity), out_shape=j...  112 us

profile of v4, /device:TPU:1, one launch (start us, length us, event | category | flops | bytes accessed | tf_op | source)
XLA Modules:
  0.0 114.3 jit_solution(7068636738345470536)
XLA Ops:
  0.0 112.0 %shard_map.55 = bf16[512,1024]{1,0:T(8,128)(2,1)} custom-call(s32[2,512]{1,0:T(2,128)} %bitcast.2, f32[2,512]{1,0:T(2,128)} %bitcast.3, bf16[512,1024]{1,0:T(8,128)(2,1)} %x_hbm.1, bf16[1,1024,1024]{2,1,0:T(8,128)(2,1)} %win_hbm.1, bf16[1,1024,1024]{2,1,0:T(8,128)(2,1)} %wout_hbm.1), custom_call_target="tpu_custom_call" | custom-call | tf_op jit(solution)/shard_map/pallas_call | solution.py:312
  112.0 2.3 %copy.7 = bf16[512,1024]{1,0:T(8,128)(2,1)} copy(bf16[512,1024]{1,0:T(8,128)(2,1)} %shard_map.55) | data formatting | bytes 2097152

commit v5 on v4

--- a/solution.py
+++ b/solution.py
@@ -13,12 +13,12 @@
 F32 = jnp.float32
 I32 = jnp.int32
 VMEM_LIMIT = 60 * 1024 * 1024
-XORDER = {4: (1, 3, 2, 0), 2: (1, 0)}
+XORDER = {4: (2, 1, 0, 3), 2: (1, 0)}
 
 
 def moe_kernel(dims, capacity, ids_hbm, gates_hbm, x_hbm, win_hbm, wout_hbm, out,
-               ids_row, gates_row, x, outbuf, inbuf, obuf, retbuf, cbuf, win, wout, st, xs, hs, acc0, acc1, tmat, tinv, rrow, rcol, wcol, flat, turned,
-               w_sem, c_send, c_recv, d_send, d_recv, r_send, r_recv):
+               ids_row, gates_row, x, outbuf, inbuf, obuf, retbuf, cbuf, win, wout, st, xs, hs, acc0, acc1, total, tmat, tinv, rrow, rcol, wcol, flat, turned,
+               w_sem, o_sem, c_send, c_recv, d_send, d_recv, r_send, r_recv):
     nz, ny, nx, nk = dims
     n = nz * ny * nx * nk
     nc, ng = nz * ny, nx * nk
@@ -276,11 +276,18 @@
     wait_group(obuf, retbuf, r_send, r_recv, last, True)
     from_wire(retbuf, last, xs)
     pick0, pick1 = picks(last)
+    leaving = []
     for b in range(4):
         part = slice(b * step, (b + 1) * step)
         first = acc0[:, part] + jnp.dot(pick0, xs[:, part], preferred_element_type=F32)
         second = acc1[:, part] + jnp.dot(pick1, xs[:, part], preferred_element_type=F32)
-        out[:, part] = (x[:, part].astype(F32) + wcol[:, 0:1] * first + wcol[:, 1:2] * second).astype(BF16)
+        total[:, part] = wcol[:, 0:1] * first + wcol[:, 1:2] * second
+        leave = pltpu.make_async_copy(total.at[:, part], out.at[:, part], o_sem.at[b])
+        leave.start()
+        leaving.append(leave)
+
+    for leave in leaving:
+        leave.wait()
 
     def drain(g, carry):
         wait_group(outbuf, inbuf, d_send, d_recv, g, False)
@@ -306,14 +313,13 @@
         wire, dense = nc * WIRE_ROWS, nc * SLOTS
         width = SLOTS * model // WIRE_ROWS
         capacity = n * (tokens * 2 // n)
-        vmem = pl.BlockSpec(memory_space=pltpu.VMEM)
         hbm = pl.BlockSpec(memory_space=pltpu.HBM)
         dma = pltpu.SemaphoreType.DMA
-        return pl.pallas_call(
+        mixed = pl.pallas_call(
             functools.partial(moe_kernel, dims, capacity),
-            out_shape=jax.ShapeDtypeStruct((tokens, model), BF16),
+            out_shape=jax.ShapeDtypeStruct((tokens, model), F32),
             in_specs=[hbm] * 5,
-            out_specs=vmem,
+            out_specs=hbm,
             scratch_shapes=[
                 pltpu.VMEM((2, tokens), I32),
                 pltpu.VMEM((2, tokens), F32),
@@ -330,6 +336,7 @@
                 pltpu.VMEM((dense, hidden), BF16),
                 pltpu.VMEM((tokens, model), F32),
                 pltpu.VMEM((tokens, model), F32),
+                pltpu.VMEM((tokens, model), F32),
                 pltpu.VMEM((wire, wire), BF16),
                 pltpu.VMEM((wire, wire), BF16),
                 pltpu.VMEM((2, tokens), I32),
@@ -337,9 +344,10 @@
                 pltpu.VMEM((tokens, 2), F32),
                 pltpu.VMEM((8, tokens), F32),
                 pltpu.VMEM((tokens, 8), F32),
-                dma((5,)), dma((1,)), dma((1,)), dma((ng,)), dma((ng,)), dma((ng,)), dma((ng,)),
+                dma((5,)), dma((4,)), dma((1,)), dma((1,)), dma((ng,)), dma((ng,)), dma((ng,)), dma((ng,)),
             ],
             compiler_params=pltpu.CompilerParams(has_side_effects=True, collective_id=0, vmem_limit_bytes=VMEM_LIMIT),
         )(expert_ids.T, gate_weights.T, token_rows, w_in, w_out)
+        return (token_rows.astype(F32) + mixed).astype(BF16)
 
     return jax.shard_map(device_step, mesh=mesh, in_specs=(row_spec, row_spec, row_spec, weight_spec, weight_spec), out_specs=row_spec, check_vma=False)

time: 114 us -> 115 us (level)
  the two profiles are of different devices: /device:TPU:1 before, /device:TPU:22 now
where the time goes in v5:
time: 115 us; the launch traced here: 114 us
  Pallas kernels  111 us (97%)
  other arithmetic  2.91 us (3%)
    pallas_call x1, Pallas kernels, device_step(): pl.pallas_call(functools.partial(moe_kernel, dims, capacity), out_shape=j...  111 us
    convert_element_type x1, other arithmetic, device_step(): return (token_rows.astype(F32) + mixed).astype(BF16)  2.91 us

profile of v5, /device:TPU:22, one launch (start us, length us, event | category | flops | bytes accessed | tf_op | source)
XLA Modules:
  0.0 114.4 jit_solution(16226091320724458860)
XLA Ops:
  0.0 0.0 copy-start
  0.0 111.5 %shard_map.55 = f32[512,1024]{1,0:T(8,128)} custom-call(s32[2,512]{1,0:T(2,128)} %bitcast.2, f32[2,512]{1,0:T(2,128)} %bitcast.3, bf16[512,1024]{1,0:T(8,128)(2,1)} %x_hbm.1, bf16[1,1024,1024]{2,1,0:T(8,128)(2,1)} %win_hbm.1, bf16[1,1024,1024]{2,1,0:T(8,128)(2,1)} %wout_hbm.1), custom_call_target="tpu_custom_call" | custom-call | tf_op jit(solution)/shard_map/pallas_call | solution.py:318
  111.5 0.0 copy-done
  111.5 2.9 %add_convert_fusion = bf16[512,1024]{1,0:T(8,128)(2,1)} fusion(f32[512,1024]{1,0:T(8,128)} %shard_map.55, bf16[512,1024]{1,0:T(8,128)(2,1)S(1)} %copy-done), kind=kLoop, calls=%fused_computation | loop fusion | flops 1572864 | bytes 4194304 | tf_op jit(solution)/shard_map/convert_element_type | solution.py:351
Async XLA Ops:
  0.0 111.5 %copy-start = (bf16[512,1024]{1,0:T(8,128)(2,1)S(1)}, bf16[512,1024]{1,0:T(8,128)(2,1)}, u32[]{:S(2)}) copy-start(bf16[512,1024]{1,0:T(8,128)(2,1)} %x_hbm.1) | copy-start | bytes 3145732

commit v6 on v4

--- a/solution.py
+++ b/solution.py
@@ -13,12 +13,12 @@
 F32 = jnp.float32
 I32 = jnp.int32
 VMEM_LIMIT = 60 * 1024 * 1024
-XORDER = {4: (1, 3, 2, 0), 2: (1, 0)}
+XORDER = {4: (2, 1, 0, 3), 2: (1, 0)}
 
 
 def moe_kernel(dims, capacity, ids_hbm, gates_hbm, x_hbm, win_hbm, wout_hbm, out,
                ids_row, gates_row, x, outbuf, inbuf, obuf, retbuf, cbuf, win, wout, st, xs, hs, acc0, acc1, tmat, tinv, rrow, rcol, wcol, flat, turned,
-               w_sem, c_send, c_recv, d_send, d_recv, r_send, r_recv):
+               w_sem, c_send, c_recv, f_send, f_recv, d_send, d_recv, r_send, r_recv):
     nz, ny, nx, nk = dims
     n = nz * ny * nx * nk
     nc, ng = nz * ny, nx * nk
@@ -189,13 +189,15 @@
         return dispatch(g, build(g, carry))
     lax.fori_loop(ng // 2, ng, build_dispatch, 0)
 
-    def send_counts(g, carry):
+    def send_counts(u, carry):
+        g = u * nk
+
         def act(c, device):
             pltpu.make_async_remote_copy(src_ref=cbuf.at[own], dst_ref=cbuf.at[g * nc + c], send_sem=c_send.at[0], recv_sem=c_recv.at[0],
                                          device_id={"expert": device}, device_id_type=pl.DeviceIdType.MESH).start()
         each_peer(g, 1, act)
         return carry
-    lax.fori_loop(0, ng, send_counts, 0)
+    lax.fori_loop(0, ng // nk, send_counts, 0)
     inbuf[own_rows, :] = outbuf[own_rows, :]
 
     later = iota((tokens, tokens), 1) < iota((tokens, tokens), 0)
@@ -231,9 +233,37 @@
     lax.fori_loop(0, ng, expert, 0)
     retbuf[own_rows, :] = obuf[own_rows, :]
 
-    pltpu.make_async_remote_copy(src_ref=cbuf.at[pl.ds(1, n - 1)], dst_ref=cbuf.at[pl.ds(1, n - 1)], send_sem=c_send.at[0], recv_sem=c_recv.at[0],
+    near = pl.ds(0, n // nk - 1)
+    pltpu.make_async_remote_copy(src_ref=cbuf.at[near], dst_ref=cbuf.at[near], send_sem=c_send.at[0], recv_sem=c_recv.at[0],
                                  device_id={"expert": me}, device_id_type=pl.DeviceIdType.MESH).wait()
-
+    hand = [pltpu.make_async_remote_copy(src_ref=cbuf.at[pl.ds(u * nk * nc, nc)], dst_ref=cbuf.at[pl.ds((u * nk + 1) * nc, nc)],
+                                         send_sem=f_send.at[u], recv_sem=f_recv.at[u],
+                                         device_id={"expert": me - mk + lax.rem(mk + 1, nk)}, device_id_type=pl.DeviceIdType.MESH)
+            for u in range(ng // nk)]
+    for copy in hand:
+        copy.start()
+
+    acc0[...] = jnp.zeros_like(acc0)
+    acc1[...] = jnp.zeros_like(acc1)
+    xs[dense:wire, :] = jnp.zeros((wire - dense, model), BF16)
+
+    def picks(g):
+        cols = iota((tokens, wire), 1)
+        wants = [rcol[:, j:j + 1] - g * dense for j in range(2)]
+        return [ones((want == cols) & (cols < dense)) for want in wants]
+
+    def combine(g, carry):
+        wait_group(obuf, retbuf, r_send, r_recv, g, True)
+        from_wire(retbuf, g, xs)
+        for pick, acc in zip(picks(g), (acc0, acc1)):
+            for b in range(4):
+                part = slice(b * step, (b + 1) * step)
+                acc[:, part] += jnp.dot(pick, xs[:, part], preferred_element_type=F32)
+        return carry
+    lax.fori_loop(0, ng // 2, combine, 0)
+
+    for copy in hand:
+        copy.wait()
     packed = cbuf[...].reshape(n, n)
     second = packed // 65536
     first = packed - second * 65536
@@ -253,24 +283,7 @@
         mine = jnp.sum(jnp.where(ids_col[:, j:j + 1] == lanes, offset, 0), axis=1, keepdims=True)
         wcol[:, j:j + 1] = jnp.where(mine + rcol[:, 2 + j:3 + j] < capacity, turned[:, 2 + j:3 + j], 0.0)
 
-    acc0[...] = jnp.zeros_like(acc0)
-    acc1[...] = jnp.zeros_like(acc1)
-    xs[dense:wire, :] = jnp.zeros((wire - dense, model), BF16)
-
-    def picks(g):
-        cols = iota((tokens, wire), 1)
-        wants = [rcol[:, j:j + 1] - g * dense for j in range(2)]
-        return [ones((want == cols) & (cols < dense)) for want in wants]
-
-    def combine(g, carry):
-        wait_group(obuf, retbuf, r_send, r_recv, g, True)
-        from_wire(retbuf, g, xs)
-        for pick, acc in zip(picks(g), (acc0, acc1)):
-            for b in range(4):
-                part = slice(b * step, (b + 1) * step)
-                acc[:, part] += jnp.dot(pick, xs[:, part], preferred_element_type=F32)
-        return carry
-    lax.fori_loop(0, ng - 1, combine, 0)
+    lax.fori_loop(ng // 2, ng - 1, combine, 0)
 
     last = ng - 1
     wait_group(obuf, retbuf, r_send, r_recv, last, True)
@@ -311,7 +324,7 @@
         dma = pltpu.SemaphoreType.DMA
         return pl.pallas_call(
             functools.partial(moe_kernel, dims, capacity),
-            out_shape=jax.ShapeDtypeStruct((tokens, model), BF16),
+            out_shape=pltpu.VMEM((tokens, model), BF16),
             in_specs=[hbm] * 5,
             out_specs=vmem,
             scratch_shapes=[
@@ -337,7 +350,7 @@
                 pltpu.VMEM((tokens, 2), F32),
                 pltpu.VMEM((8, tokens), F32),
                 pltpu.VMEM((tokens, 8), F32),
-                dma((5,)), dma((1,)), dma((1,)), dma((ng,)), dma((ng,)), dma((ng,)), dma((ng,)),
+                dma((5,)), dma((1,)), dma((1,)), dma((ng // dims[3],)), dma((ng // dims[3],)), dma((ng,)), dma((ng,)), dma((ng,)), dma((ng,)),
             ],
             compiler_params=pltpu.CompilerParams(has_side_effects=True, collective_id=0, vmem_limit_bytes=VMEM_LIMIT),
         )(expert_ids.T, gate_weights.T, token_rows, w_in, w_out)

time: 114 us -> 110 us (0.965)
  the two profiles are of different devices: /device:TPU:1 before, /device:TPU:29 now
where the time goes in v6:
time: 110 us
  Pallas kernels  109 us (99%)
    pallas_call x1, Pallas kernels, device_step(): pl.pallas_call(functools.partial(moe_kernel, dims, capacity), out_shape=p...  109 us

profile of v6, /device:TPU:29, one launch (start us, length us, event | category | flops | bytes accessed | tf_op | source)
XLA Modules:
  0.0 109.9 jit_solution(13306586713680065277)
XLA Ops:
  0.0 108.9 %shard_map.55 = bf16[512,1024]{1,0:T(8,128)(2,1)S(1)} custom-call(s32[2,512]{1,0:T(2,128)} %bitcast.2, f32[2,512]{1,0:T(2,128)} %bitcast.3, bf16[512,1024]{1,0:T(8,128)(2,1)} %x_hbm.1, bf16[1,1024,1024]{2,1,0:T(8,128)(2,1)} %win_hbm.1, bf16[1,1024,1024]{2,1,0:T(8,128)(2,1)} %wout_hbm.1), custom_call_target="tpu_custom_call" | custom-call | tf_op jit(solution)/shard_map/pallas_call | solution.py:325
  108.9 1.0 copy.7

commit v7 on v6

--- a/solution.py
+++ b/solution.py
@@ -110,7 +110,9 @@
     def hello(i, carry):
         pl.semaphore_signal(barrier, inc=1, device_id={"expert": lax.rem(me + i, n)}, device_id_type=pl.DeviceIdType.MESH)
         return carry
-    lax.fori_loop(1, n, hello, 0, unroll=4)
+    far = n // 2 - n // 32
+    lax.fori_loop(far, n, hello, 0, unroll=4)
+    lax.fori_loop(1, far, hello, 0, unroll=4)
     fetch[0].wait()
     fetch[1].wait()
 
@@ -214,6 +216,9 @@
     rcol[:, 2:3] = rank0
     rcol[:, 3:4] = rank1
 
+    acc0[...] = jnp.zeros_like(acc0)
+    acc1[...] = jnp.zeros_like(acc1)
+    xs[dense:wire, :] = jnp.zeros((wire - dense, model), BF16)
     fetch[3].wait()
     fetch[4].wait()
 
@@ -243,9 +248,6 @@
     for copy in hand:
         copy.start()
 
-    acc0[...] = jnp.zeros_like(acc0)
-    acc1[...] = jnp.zeros_like(acc1)
-    xs[dense:wire, :] = jnp.zeros((wire - dense, model), BF16)
 
     def picks(g):
         cols = iota((tokens, wire), 1)

time: 110 us -> 114 us (1.036)
  the two profiles are of different devices: /device:TPU:29 before, /device:TPU:2 now
where the time goes in v7:
time: 114 us
  Pallas kernels  113 us (99%)
    pallas_call x1, Pallas kernels, device_step(): pl.pallas_call(functools.partial(moe_kernel, dims, capacity), out_shape=p...  113 us

profile of v7, /device:TPU:2, one launch (start us, length us, event | category | flops | bytes accessed | tf_op | source)
XLA Modules:
  0.0 113.5 jit_solution(16631856390164353780)
XLA Ops:
  0.0 112.5 %shard_map.55 = bf16[512,1024]{1,0:T(8,128)(2,1)S(1)} custom-call(s32[2,512]{1,0:T(2,128)} %bitcast.2, f32[2,512]{1,0:T(2,128)} %bitcast.3, bf16[512,1024]{1,0:T(8,128)(2,1)} %x_hbm.1, bf16[1,1024,1024]{2,1,0:T(8,128)(2,1)} %win_hbm.1, bf16[1,1024,1024]{2,1,0:T(8,128)(2,1)} %wout_hbm.1), custom_call_target="tpu_custom_call" | custom-call | tf_op jit(solution)/shard_map/pallas_call | solution.py:327
  112.5 1.0 copy.7
